TPU v7x, 768 devices: a whole 4x8x12 slice. The times are simulated.
768 devices in a mesh: gx: 16 (over y, x_lo), gy: 4 (over x_hi, core), gz: 12 (over z).
Axes of the slice: x: 4 (x_hi: 2, x_lo: 2; x = x_hi * 2 + x_lo), y: 8, z: 12, core: 2. Of those that a mesh axis runs over, the one named last changes fastest.
Arguments:
- flow_state: float32 [6, 64, 64, 1536], P(None, 'gx', 'gy', 'gz'), may hold values from -6 to 6
Outputs:
- new_vorticity: float32 [3, 64, 64, 1536], P(None, 'gx', 'gy', 'gz')
All inputs are finite; a program needn't handle non-finite values.
Results may differ from a plain program's by a relative error of at most 0.0001.
Values sent between devices are 32-bit elements; how exact they have to be, the bound alone decides.
No kernel may reach another device: no remote copies, remote signals or barrier semaphores. Data moves between devices by JAX's collectives and lax.ppermute only.
A program may use at most 64 MiB of HBM per device.

v0:
```python
import functools

import jax
import jax.numpy as jnp
from jax import lax
from jax.sharding import Mesh
from jax.sharding import PartitionSpec as P

GX = ("gx_0", "gx_1")
GY = ("gy_0", "gy_1")
GX_GY_GZ = ("gx_0", "gx_1", "gy_0", "gy_1", "gz")


def extended(array, sides, width):
    for axis, dim in sides:
        count, length = (lax.axis_size(axis), array.shape[dim])
        up = [(i, (i + 1) % count) for i in range(count)]
        down = [(j, i) for i, j in up]
        last = lax.slice_in_dim(array, length - width, length, axis=dim)
        initial = lax.slice_in_dim(array, 0, width, axis=dim)
        before = lax.ppermute(last, axis, up)
        after = lax.ppermute(initial, axis, down)
        array = jnp.concatenate([before, array, after], axis=dim)
    return array


def over_axes(array, axes):
    return functools.reduce(lax.pmax, axes, array)


def window(values, dimension, offset, length):
    return lax.slice_in_dim(values, offset, offset + length, axis=dimension)


def derivatives(padded, dimension, length):
    minus_two = window(padded, dimension, 0, length)
    minus_one = window(padded, dimension, 1, length)
    center = window(padded, dimension, 2, length)
    plus_one = window(padded, dimension, 3, length)
    plus_two = window(padded, dimension, 4, length)
    gradient = (8.0 * (plus_one[3:6] - minus_one[3:6]) - (plus_two[3:6] - minus_two[3:6])) / 12.0
    curvature = (
        16.0 * (plus_one[0:3] + minus_one[0:3])
        - (plus_two[0:3] + minus_two[0:3])
        - 30.0 * center[0:3]
    ) / 12.0
    return (gradient, curvature)


def on_device(flow_state):
    extent = flow_state.shape[1:]
    slabs = [
        extended(flow_state, ((GX, 1),), 2),
        extended(flow_state, ((GY, 2),), 2),
        extended(flow_state, (("gz", 3),), 2),
    ]
    vorticity = flow_state[0:3]
    gradients = []
    laplace = jnp.zeros_like(vorticity)
    for dimension in range(3):
        gradient, curvature = derivatives(slabs[dimension], dimension + 1, extent[dimension])
        gradients.append(gradient)
        laplace = laplace + curvature
    strain = jnp.zeros(extent, jnp.float32)
    for gradient in gradients:
        strain = strain + jnp.sum(gradient * gradient, axis=0)
    peak = over_axes(jnp.max(strain), GX_GY_GZ)
    step_size = 0.25 / jnp.maximum(1.0, jnp.sqrt(peak))
    stretch = jnp.zeros_like(vorticity)
    for dimension in range(3):
        stretch = stretch + vorticity[dimension : dimension + 1] * gradients[dimension]
    return vorticity + step_size * (stretch + 0.5 * laplace)


def solution(mesh):
    finer = Mesh(
        mesh.devices.reshape(8, 2, 2, 2, mesh.shape["gz"]), ("gx_0", "gx_1", "gy_0", "gy_1", "gz")
    )
    placed = (P(None, GX, GY, "gz"),)
    return jax.shard_map(
        on_device, mesh=finer, in_specs=placed, out_specs=P(None, GX, GY, "gz"), check_vma=False
    )
```

profile of v0, /device:TPU:2, one launch (start us, length us, event | category | flops | bytes accessed | tf_op | source)
XLA Modules:
  0.0 95.9 jit_solution(17289483419110467908)
XLA Ops:
  0.0 0.0 copy-start
  0.0 1.0 %fusion.37 = (f32[6,2,16,128]{3,2,1,0:T(8,128)S(1)}, f32[6,2,16,128]{3,2,1,0:T(8,128)S(1)}) fusion(f32[6,4,16,128]{3,2,1,0:T(8,128)} %param.1), kind=kLoop, calls=%fused_computation.68 | loop fusion | bytes 393216 | tf_op jit(solution)/shard_map/slice | solution.py:20
  1.0 3.5 %collective-permute-start.1 = (f32[6,2,16,128]{3,2,1,0:T(8,128)S(1)}, f32[6,2,16,128]{3,2,1,0:T(8,128)S(1)}, u32[]{:S(2)}, u32[]{:S(2)}) collective-permute-start(f32[6,2,16,128]{3,2,1,0:T(8,128)S(1)} %get-tuple-element.17), channel_id=1, source_target_pairs={{0,48},{48,96},{96,144},{144,192},{192,240},{240,288},{288,336},{3... | collective-permute-start | bytes 294920 | tf_op jit(solution)/shard_map/ppermute | solution.py:21
  4.5 0.0 copy-done
  4.5 0.1 fusion.39
  4.6 14.6 %collective-permute-start.4 = (f32[6,4,16,2]{3,2,1,0:T(8,128)S(1)}, f32[6,4,16,2]{3,2,1,0:T(8,128)S(1)}, u32[]{:S(2)}, u32[]{:S(2)}) collective-permute-start(f32[6,4,16,2]{3,2,1,0:T(8,128)S(1)} %get-tuple-element.24), channel_id=1, source_target_pairs={{1,0},{2,1},{3,2},{4,3},{5,4},{6,5},{7,6},{8,7},{9,8},{10,9},{11,1... | collective-permute-start | bytes 9224 | tf_op jit(solution)/shard_map/ppermute | solution.py:22
  19.2 3.2 %collective-permute-start.2 = (f32[6,4,2,128]{3,2,1,0:T(2,128)S(1)}, f32[6,4,2,128]{3,2,1,0:T(2,128)S(1)}, u32[]{:S(2)}, u32[]{:S(2)}) collective-permute-start(f32[6,4,2,128]{3,2,1,0:T(2,128)S(1)} %get-tuple-element.22), channel_id=1, source_target_pairs={{12,0},{24,12},{36,24},{0,36},{13,1},{25,13},{37,25},{1,37},{14,2}... | collective-permute-start | bytes 73736 | tf_op jit(solution)/shard_map/ppermute | solution.py:22
  22.4 1.9 %collective-permute-start.5 = (f32[6,4,16,2]{3,2,1,0:T(8,128)S(1)}, f32[6,4,16,2]{3,2,1,0:T(8,128)S(1)}, u32[]{:S(2)}, u32[]{:S(2)}) collective-permute-start(f32[6,4,16,2]{3,2,1,0:T(8,128)S(1)} %get-tuple-element.25), channel_id=1, source_target_pairs={{0,1},{1,2},{2,3},{3,4},{4,5},{5,6},{6,7},{7,8},{8,9},{9,10},{10,1... | collective-permute-start | bytes 9224 | tf_op jit(solution)/shard_map/ppermute | solution.py:21
  24.4 1.9 %collective-permute-start.3 = (f32[6,4,2,128]{3,2,1,0:T(2,128)S(1)}, f32[6,4,2,128]{3,2,1,0:T(2,128)S(1)}, u32[]{:S(2)}, u32[]{:S(2)}) collective-permute-start(f32[6,4,2,128]{3,2,1,0:T(2,128)S(1)} %get-tuple-element.23), channel_id=1, source_target_pairs={{0,12},{12,24},{24,36},{36,0},{1,13},{13,25},{25,37},{37,1},{2,14}... | collective-permute-start | bytes 73736 | tf_op jit(solution)/shard_map/ppermute | solution.py:21
  26.3 0.0 collective-permute-done.1
  26.3 2.7 %collective-permute-start = (f32[6,2,16,128]{3,2,1,0:T(8,128)S(1)}, f32[6,2,16,128]{3,2,1,0:T(8,128)S(1)}, u32[]{:S(2)}, u32[]{:S(2)}) collective-permute-start(f32[6,2,16,128]{3,2,1,0:T(8,128)S(1)} %get-tuple-element.16), channel_id=1, source_target_pairs={{48,0},{96,48},{144,96},{192,144},{240,192},{288,240},{336,288},{3... | collective-permute-start | bytes 294920 | tf_op jit(solution)/shard_map/ppermute | solution.py:22
  29.0 0.1 constant_dynamic-update-slice_fusion.1
  29.1 5.4 %collective-permute-done = f32[6,2,16,128]{3,2,1,0:T(8,128)S(1)} collective-permute-done((f32[6,2,16,128]{3,2,1,0:T(8,128)S(1)}, f32[6,2,16,128]{3,2,1,0:T(8,128)S(1)}, u32[]{:S(2)}, u32[]{:S(2)}) %collective-permute-start) | collective-permute-done | bytes 98336 | tf_op jit(solution)/shard_map/ppermute | solution.py:22
  34.5 0.0 collective-permute-done.4
  34.6 0.0 collective-permute-done.2
  34.6 0.0 collective-permute-done.5
  34.6 0.0 collective-permute-done.3
  34.6 0.2 multiply_reduce_fusion.1
  34.8 0.6 add_reduce_fusion
  35.4 18.7 %pmax.35 = f32[]{:T(128)} all-reduce(f32[]{:T(128)} %add_reduce_fusion), channel_id=1, replica_groups=mesh['gx_0'=8,'gx_1'=2,'gy_0'=2,'gy_1'=2,'gz'=12] {'gx_0'}, use_global_device_ids=true, to_apply=%region_4.0 | all-reduce | flops 1 | bytes 8 | tf_op jit(solution)/shard_map/pmax | solution.py:28
  54.1 5.6 %pmax.36 = f32[]{:T(128)} all-reduce(f32[]{:T(128)} %pmax.35), channel_id=1, replica_groups=mesh['gx_0'=8,'gx_1'=2,'gy_0'=2,'gy_1'=2,'gz'=12] {'gx_1'}, use_global_device_ids=true, to_apply=%region_5.0 | all-reduce | flops 1 | bytes 8 | tf_op jit(solution)/shard_map/pmax | solution.py:28
  59.7 7.1 %pmax.37 = f32[]{:T(128)} all-reduce(f32[]{:T(128)} %pmax.36), channel_id=1, replica_groups=mesh['gx_0'=8,'gx_1'=2,'gy_0'=2,'gy_1'=2,'gz'=12] {'gy_0'}, use_global_device_ids=true, to_apply=%region_6.0 | all-reduce | flops 1 | bytes 8 | tf_op jit(solution)/shard_map/pmax | solution.py:28
  66.7 3.1 %pmax.38 = f32[]{:T(128)} all-reduce(f32[]{:T(128)} %pmax.37), channel_id=1, replica_groups=mesh['gx_0'=8,'gx_1'=2,'gy_0'=2,'gy_1'=2,'gz'=12] {'gy_1'}, use_global_device_ids=true, to_apply=%region_7.0 | all-reduce | flops 1 | bytes 8 | tf_op jit(solution)/shard_map/pmax | solution.py:28
  69.8 24.5 %pmax.39 = f32[]{:T(128)} all-reduce(f32[]{:T(128)} %pmax.38), channel_id=1, replica_groups=mesh['gx_0'=8,'gx_1'=2,'gy_0'=2,'gy_1'=2,'gz'=12] {'gz'}, use_global_device_ids=true, to_apply=%region_8.0 | all-reduce | flops 1 | bytes 8 | tf_op jit(solution)/shard_map/pmax | solution.py:28
  95.0 0.9 fusion.10
  (7 shorter events, 0.1 us)
Async XLA Ops:
  0.0 4.5 %copy-start = (f32[6,4,16,128]{3,2,1,0:T(8,128)S(1)}, f32[6,4,16,128]{3,2,1,0:T(8,128)}, u32[]{:S(2)}) copy-start(f32[6,4,16,128]{3,2,1,0:T(8,128)} %param.1) | copy-start | bytes 589828
  1.0 25.3 %collective-permute-start.1 = (f32[6,2,16,128]{3,2,1,0:T(8,128)S(1)}, f32[6,2,16,128]{3,2,1,0:T(8,128)S(1)}, u32[]{:S(2)}, u32[]{:S(2)}) collective-permute-start(f32[6,2,16,128]{3,2,1,0:T(8,128)S(1)} %get-tuple-element.17), channel_id=1, source_target_pairs={{0,48},{48,96},{96,144},{144,192},{192,240},{240,288},{288,336},{3... | collective-permute-start | bytes 294920 | tf_op jit(solution)/shard_map/ppermute | solution.py:21
  4.6 29.9 %collective-permute-start.4 = (f32[6,4,16,2]{3,2,1,0:T(8,128)S(1)}, f32[6,4,16,2]{3,2,1,0:T(8,128)S(1)}, u32[]{:S(2)}, u32[]{:S(2)}) collective-permute-start(f32[6,4,16,2]{3,2,1,0:T(8,128)S(1)} %get-tuple-element.24), channel_id=1, source_target_pairs={{1,0},{2,1},{3,2},{4,3},{5,4},{6,5},{7,6},{8,7},{9,8},{10,9},{11,1... | collective-permute-start | bytes 9224 | tf_op jit(solution)/shard_map/ppermute | solution.py:22
  19.2 15.4 %collective-permute-start.2 = (f32[6,4,2,128]{3,2,1,0:T(2,128)S(1)}, f32[6,4,2,128]{3,2,1,0:T(2,128)S(1)}, u32[]{:S(2)}, u32[]{:S(2)}) collective-permute-start(f32[6,4,2,128]{3,2,1,0:T(2,128)S(1)} %get-tuple-element.22), channel_id=1, source_target_pairs={{12,0},{24,12},{36,24},{0,36},{13,1},{25,13},{37,25},{1,37},{14,2}... | collective-permute-start | bytes 73736 | tf_op jit(solution)/shard_map/ppermute | solution.py:22
  22.4 12.2 %collective-permute-start.5 = (f32[6,4,16,2]{3,2,1,0:T(8,128)S(1)}, f32[6,4,16,2]{3,2,1,0:T(8,128)S(1)}, u32[]{:S(2)}, u32[]{:S(2)}) collective-permute-start(f32[6,4,16,2]{3,2,1,0:T(8,128)S(1)} %get-tuple-element.25), channel_id=1, source_target_pairs={{0,1},{1,2},{2,3},{3,4},{4,5},{5,6},{6,7},{7,8},{8,9},{9,10},{10,1... | collective-permute-start | bytes 9224 | tf_op jit(solution)/shard_map/ppermute | solution.py:21
  24.4 10.3 %collective-permute-start.3 = (f32[6,4,2,128]{3,2,1,0:T(2,128)S(1)}, f32[6,4,2,128]{3,2,1,0:T(2,128)S(1)}, u32[]{:S(2)}, u32[]{:S(2)}) collective-permute-start(f32[6,4,2,128]{3,2,1,0:T(2,128)S(1)} %get-tuple-element.23), channel_id=1, source_target_pairs={{0,12},{12,24},{24,36},{36,0},{1,13},{13,25},{25,37},{37,1},{2,14}... | collective-permute-start | bytes 73736 | tf_op jit(solution)/shard_map/ppermute | solution.py:21
  26.3 8.2 %collective-permute-start = (f32[6,2,16,128]{3,2,1,0:T(8,128)S(1)}, f32[6,2,16,128]{3,2,1,0:T(8,128)S(1)}, u32[]{:S(2)}, u32[]{:S(2)}) collective-permute-start(f32[6,2,16,128]{3,2,1,0:T(8,128)S(1)} %get-tuple-element.16), channel_id=1, source_target_pairs={{48,0},{96,48},{144,96},{192,144},{240,192},{288,240},{336,288},{3... | collective-permute-start | bytes 294920 | tf_op jit(solution)/shard_map/ppermute | solution.py:22
where the time goes:
time: 96.3 us; the launch traced here: 95.9 us
  blocking collectives  58.8 us (61%)
  starting transfers between devices  27.8 us (29%)
  waiting for transfers between devices  5.41 us (6%)
  other arithmetic  1.7 us (2%)
  local copies, waits for them, and re-layouts  1.24 us (1%)
    pmax x5, blocking collectives, over_axes(): return functools.reduce(lax.pmax, axes, array)  58.8 us
    ppermute x3, starting transfers between devices, extended(): after = lax.ppermute(initial, axis, down)  20.5 us
    ppermute x3, starting transfers between devices, extended(): before = lax.ppermute(last, axis, up)  7.3 us
    ppermute x3, waiting for transfers between devices, extended(): after = lax.ppermute(initial, axis, down)  5.41 us
  transfers between devices with their start and end apart: 6, of which 1 were waited for; matrix products, arithmetic and copies ran while one was open for 0% of the time, Pallas kernels for 0%

commit v1 on v0

--- a/solution.py
+++ b/solution.py
@@ -1,5 +1,3 @@
-import functools
-
 import jax
 import jax.numpy as jnp
 from jax import lax
@@ -8,7 +6,8 @@
 
 GX = ("gx_0", "gx_1")
 GY = ("gy_0", "gy_1")
-GX_GY_GZ = ("gx_0", "gx_1", "gy_0", "gy_1", "gz")
+LINE = ("gy_1", "gz")
+PLANE = ("gx_0", "gx_1", "gy_0")
 
 
 def extended(array, sides, width):
@@ -24,8 +23,13 @@
     return array
 
 
-def over_axes(array, axes):
-    return functools.reduce(lax.pmax, axes, array)
+def peak_of(strain):
+    lanes = jnp.max(strain, axis=(0, 1)).reshape(1, 1, -1)
+    for axes in (LINE, PLANE):
+        count = lax.axis_size(axes)
+        sent = jnp.broadcast_to(lanes, (count,) + lanes.shape[1:])
+        lanes = jnp.max(lax.all_to_all(sent, axes, 0, 0, tiled=True), axis=0, keepdims=True)
+    return jnp.max(lanes)
 
 
 def window(values, dimension, offset, length):
@@ -64,7 +68,7 @@
     strain = jnp.zeros(extent, jnp.float32)
     for gradient in gradients:
         strain = strain + jnp.sum(gradient * gradient, axis=0)
-    peak = over_axes(jnp.max(strain), GX_GY_GZ)
+    peak = peak_of(strain)
     step_size = 0.25 / jnp.maximum(1.0, jnp.sqrt(peak))
     stretch = jnp.zeros_like(vorticity)
     for dimension in range(3):

time: 96.3 us -> 71.9 us (0.75)
  the two profiles are of different devices: /device:TPU:2 before, /device:TPU:1 now
where the time goes in v1:
time: 71.9 us; the launch traced here: 71.5 us
  starting transfers between devices  41.4 us (58%)
  blocking collectives  15 us (21%)
  waiting for transfers between devices  10.5 us (15%)
  local copies, waits for them, and re-layouts  1.87 us (3%)
  other arithmetic  1.74 us (2%)
  between operations  0.91 us (1%)
    ppermute x3, starting transfers between devices, extended(): after = lax.ppermute(initial, axis, down)  21.9 us
    all_to_all x1, blocking collectives, peak_of(): lax.all_to_all(sent, axes, 0, 0, tiled=True)  15 us
    ppermute x3, starting transfers between devices, extended(): before = lax.ppermute(last, axis, up)  10.1 us
    all_to_all x1, starting transfers between devices, peak_of(): lax.all_to_all(sent, axes, 0, 0, tiled=True)  9.33 us
    all_to_all x1, waiting for transfers between devices, peak_of(): lax.all_to_all(sent, axes, 0, 0, tiled=True)  8.56 us
    ppermute x3, waiting for transfers between devices, extended(): after = lax.ppermute(initial, axis, down)  1.97 us
  transfers between devices with their start and end apart: 7, of which 2 were waited for; matrix products, arithmetic and copies ran while one was open for 0% of the time, Pallas kernels for 0%

profile of v1, /device:TPU:1, one launch (start us, length us, event | category | flops | bytes accessed | tf_op | source)
XLA Modules:
  0.0 71.5 jit_solution(3673820452996342300)
XLA Ops:
  0.0 0.0 copy-start
  0.0 1.0 %fusion.37 = (f32[6,2,16,128]{3,2,1,0:T(8,128)S(1)}, f32[6,2,16,128]{3,2,1,0:T(8,128)S(1)}) fusion(f32[6,4,16,128]{3,2,1,0:T(8,128)} %param.1), kind=kLoop, calls=%fused_computation.68 | loop fusion | bytes 393216 | tf_op jit(solution)/shard_map/slice | solution.py:19
  1.0 3.9 %collective-permute-start.1 = (f32[6,2,16,128]{3,2,1,0:T(8,128)S(1)}, f32[6,2,16,128]{3,2,1,0:T(8,128)S(1)}, u32[]{:S(2)}, u32[]{:S(2)}) collective-permute-start(f32[6,2,16,128]{3,2,1,0:T(8,128)S(1)} %get-tuple-element.17), channel_id=1, source_target_pairs={{0,48},{48,96},{96,144},{144,192},{192,240},{240,288},{288,336},{3... | collective-permute-start | bytes 294920 | tf_op jit(solution)/shard_map/ppermute | solution.py:20
  4.9 0.0 copy-done
  5.0 0.1 fusion.39
  5.1 14.3 %collective-permute-start.4 = (f32[6,4,16,2]{3,2,1,0:T(8,128)S(1)}, f32[6,4,16,2]{3,2,1,0:T(8,128)S(1)}, u32[]{:S(2)}, u32[]{:S(2)}) collective-permute-start(f32[6,4,16,2]{3,2,1,0:T(8,128)S(1)} %get-tuple-element.24), channel_id=1, source_target_pairs={{1,0},{2,1},{3,2},{4,3},{5,4},{6,5},{7,6},{8,7},{9,8},{10,9},{11,1... | collective-permute-start | bytes 9224 | tf_op jit(solution)/shard_map/ppermute | solution.py:21
  19.4 3.1 %collective-permute-start.2 = (f32[6,4,2,128]{3,2,1,0:T(2,128)S(1)}, f32[6,4,2,128]{3,2,1,0:T(2,128)S(1)}, u32[]{:S(2)}, u32[]{:S(2)}) collective-permute-start(f32[6,4,2,128]{3,2,1,0:T(2,128)S(1)} %get-tuple-element.22), channel_id=1, source_target_pairs={{12,0},{24,12},{36,24},{0,36},{13,1},{25,13},{37,25},{1,37},{14,2}... | collective-permute-start | bytes 73736 | tf_op jit(solution)/shard_map/ppermute | solution.py:21
  22.6 1.9 %collective-permute-start.5 = (f32[6,4,16,2]{3,2,1,0:T(8,128)S(1)}, f32[6,4,16,2]{3,2,1,0:T(8,128)S(1)}, u32[]{:S(2)}, u32[]{:S(2)}) collective-permute-start(f32[6,4,16,2]{3,2,1,0:T(8,128)S(1)} %get-tuple-element.25), channel_id=1, source_target_pairs={{0,1},{1,2},{2,3},{3,4},{4,5},{5,6},{6,7},{7,8},{8,9},{9,10},{10,1... | collective-permute-start | bytes 9224 | tf_op jit(solution)/shard_map/ppermute | solution.py:20
  24.5 4.3 %collective-permute-start.3 = (f32[6,4,2,128]{3,2,1,0:T(2,128)S(1)}, f32[6,4,2,128]{3,2,1,0:T(2,128)S(1)}, u32[]{:S(2)}, u32[]{:S(2)}) collective-permute-start(f32[6,4,2,128]{3,2,1,0:T(2,128)S(1)} %get-tuple-element.23), channel_id=1, source_target_pairs={{0,12},{12,24},{24,36},{36,0},{1,13},{13,25},{25,37},{37,1},{2,14}... | collective-permute-start | bytes 73736 | tf_op jit(solution)/shard_map/ppermute | solution.py:20
  28.8 0.0 collective-permute-done.1
  28.8 4.5 %collective-permute-start = (f32[6,2,16,128]{3,2,1,0:T(8,128)S(1)}, f32[6,2,16,128]{3,2,1,0:T(8,128)S(1)}, u32[]{:S(2)}, u32[]{:S(2)}) collective-permute-start(f32[6,2,16,128]{3,2,1,0:T(8,128)S(1)} %get-tuple-element.16), channel_id=1, source_target_pairs={{48,0},{96,48},{144,96},{192,144},{240,192},{288,240},{336,288},{3... | collective-permute-start | bytes 294920 | tf_op jit(solution)/shard_map/ppermute | solution.py:21
  33.3 0.1 constant_dynamic-update-slice_fusion.1
  33.4 2.0 %collective-permute-done = f32[6,2,16,128]{3,2,1,0:T(8,128)S(1)} collective-permute-done((f32[6,2,16,128]{3,2,1,0:T(8,128)S(1)}, f32[6,2,16,128]{3,2,1,0:T(8,128)S(1)}, u32[]{:S(2)}, u32[]{:S(2)}) %collective-permute-start) | collective-permute-done | bytes 98336 | tf_op jit(solution)/shard_map/ppermute | solution.py:21
  35.4 0.0 collective-permute-done.4
  35.4 0.0 collective-permute-done.2
  35.4 0.0 collective-permute-done.5
  35.4 0.0 collective-permute-done.3
  35.5 0.2 multiply_reduce_fusion.1
  35.7 15.0 %all_to_all.10 = f32[24,1,128]{2,1,0:T(1,128)S(1)} all-to-all(f32[24,1,128]{2,1,0:T(1,128)S(1)} %broadcast_in_dim.4), channel_id=1, replica_groups=mesh['gx_0'=8,'gx_1'=2,'gy_0'=2,'gy_1'=2,'gz'=12] {'gy_1','gz'}, dimensions={0} | all-to-all | bytes 24576 | tf_op jit(solution)/shard_map/all_to_all | solution.py:31
  50.7 0.6 broadcast_in_dim.5
  51.3 9.3 %all-to-all-start.1 = ((f32[32,1,128]{2,1,0:T(1,128)}), f32[32,1,128]{2,1,0:T(1,128)S(1)}, u32[]{:S(2)}, u32[]{:S(2)}) async-start(f32[32,1,128]{2,1,0:T(1,128)} %broadcast_in_dim.5), calls=%async_computation.1 | async-start | bytes 32768 | tf_op jit(solution)/shard_map/all_to_all | solution.py:31
  60.7 8.6 %all-to-all-done.1 = f32[32,1,128]{2,1,0:T(1,128)S(1)} async-done(((f32[32,1,128]{2,1,0:T(1,128)}), f32[32,1,128]{2,1,0:T(1,128)S(1)}, u32[]{:S(2)}, u32[]{:S(2)}) %all-to-all-start.1) | async-done | bytes 16416 | tf_op jit(solution)/shard_map/all_to_all | solution.py:31
  69.3 0.6 reduce_max.33
  70.6 0.8 %fusion.10 = f32[3,4,16,128]{3,2,1,0:T(8,128)} fusion(f32[6,4,16,128]{3,2,1,0:T(8,128)S(1)} %copy-done, f32[6,4,2,128]{3,2,1,0:T(2,128)S(1)} %collective-permute-done.3, f32[6,4,16,2]{3,2,1,0:T(8,128)S(1)} %collective-permute-done.5, f32[6,4,16,130]{3,2,1,0:T(8,128)S(1)} %constant_dynamic-update-slice_fusion.6, ...), kind=kLoop, calls=%fused_computation.22 | loop fusion | flops 761856 | bytes 1794052 | tf_op jit(solution)/shard_map/add | solution.py:76
  (10 shorter events, 0.2 us)
Async XLA Ops:
  0.0 4.9 %copy-start = (f32[6,4,16,128]{3,2,1,0:T(8,128)S(1)}, f32[6,4,16,128]{3,2,1,0:T(8,128)}, u32[]{:S(2)}) copy-start(f32[6,4,16,128]{3,2,1,0:T(8,128)} %param.1) | copy-start | bytes 589828
  1.0 27.8 %collective-permute-start.1 = (f32[6,2,16,128]{3,2,1,0:T(8,128)S(1)}, f32[6,2,16,128]{3,2,1,0:T(8,128)S(1)}, u32[]{:S(2)}, u32[]{:S(2)}) collective-permute-start(f32[6,2,16,128]{3,2,1,0:T(8,128)S(1)} %get-tuple-element.17), channel_id=1, source_target_pairs={{0,48},{48,96},{96,144},{144,192},{192,240},{240,288},{288,336},{3... | collective-permute-start | bytes 294920 | tf_op jit(solution)/shard_map/ppermute | solution.py:20
  5.1 30.3 %collective-permute-start.4 = (f32[6,4,16,2]{3,2,1,0:T(8,128)S(1)}, f32[6,4,16,2]{3,2,1,0:T(8,128)S(1)}, u32[]{:S(2)}, u32[]{:S(2)}) collective-permute-start(f32[6,4,16,2]{3,2,1,0:T(8,128)S(1)} %get-tuple-element.24), channel_id=1, source_target_pairs={{1,0},{2,1},{3,2},{4,3},{5,4},{6,5},{7,6},{8,7},{9,8},{10,9},{11,1... | collective-permute-start | bytes 9224 | tf_op jit(solution)/shard_map/ppermute | solution.py:21
  19.4 16.0 %collective-permute-start.2 = (f32[6,4,2,128]{3,2,1,0:T(2,128)S(1)}, f32[6,4,2,128]{3,2,1,0:T(2,128)S(1)}, u32[]{:S(2)}, u32[]{:S(2)}) collective-permute-start(f32[6,4,2,128]{3,2,1,0:T(2,128)S(1)} %get-tuple-element.22), channel_id=1, source_target_pairs={{12,0},{24,12},{36,24},{0,36},{13,1},{25,13},{37,25},{1,37},{14,2}... | collective-permute-start | bytes 73736 | tf_op jit(solution)/shard_map/ppermute | solution.py:21
  22.6 12.9 %collective-permute-start.5 = (f32[6,4,16,2]{3,2,1,0:T(8,128)S(1)}, f32[6,4,16,2]{3,2,1,0:T(8,128)S(1)}, u32[]{:S(2)}, u32[]{:S(2)}) collective-permute-start(f32[6,4,16,2]{3,2,1,0:T(8,128)S(1)} %get-tuple-element.25), channel_id=1, source_target_pairs={{0,1},{1,2},{2,3},{3,4},{4,5},{5,6},{6,7},{7,8},{8,9},{9,10},{10,1... | collective-permute-start | bytes 9224 | tf_op jit(solution)/shard_map/ppermute | solution.py:20
  24.5 10.9 %collective-permute-start.3 = (f32[6,4,2,128]{3,2,1,0:T(2,128)S(1)}, f32[6,4,2,128]{3,2,1,0:T(2,128)S(1)}, u32[]{:S(2)}, u32[]{:S(2)}) collective-permute-start(f32[6,4,2,128]{3,2,1,0:T(2,128)S(1)} %get-tuple-element.23), channel_id=1, source_target_pairs={{0,12},{12,24},{24,36},{36,0},{1,13},{13,25},{25,37},{37,1},{2,14}... | collective-permute-start | bytes 73736 | tf_op jit(solution)/shard_map/ppermute | solution.py:20
  28.8 6.6 %collective-permute-start = (f32[6,2,16,128]{3,2,1,0:T(8,128)S(1)}, f32[6,2,16,128]{3,2,1,0:T(8,128)S(1)}, u32[]{:S(2)}, u32[]{:S(2)}) collective-permute-start(f32[6,2,16,128]{3,2,1,0:T(8,128)S(1)} %get-tuple-element.16), channel_id=1, source_target_pairs={{48,0},{96,48},{144,96},{192,144},{240,192},{288,240},{336,288},{3... | collective-permute-start | bytes 294920 | tf_op jit(solution)/shard_map/ppermute | solution.py:21
  51.3 17.9 %all-to-all-start.1 = ((f32[32,1,128]{2,1,0:T(1,128)}), f32[32,1,128]{2,1,0:T(1,128)S(1)}, u32[]{:S(2)}, u32[]{:S(2)}) async-start(f32[32,1,128]{2,1,0:T(1,128)} %broadcast_in_dim.5), calls=%async_computation.1 | async-start | bytes 32768 | tf_op jit(solution)/shard_map/all_to_all | solution.py:31
